TPU v7x, 16 devices: a whole 2x2x2 slice. The times are simulated.
16 devices in a mesh: fsdp: 16 (over z, y, x, core).
Axes of the slice: x: 2, y: 2, z: 2, core: 2. Of those that a mesh axis runs over, the one named last changes fastest.
Arguments:
- patches: bfloat16 [1024, 196, 768], P('fsdp')
- keep: int32 [1024, 49], P('fsdp')
- w_patch: float32 [768, 1024], P(None, 'fsdp')
- b_patch: float32 [1024], P('fsdp')
- pos_table: float32 [197, 1024], P(None, 'fsdp')
- cls_tok: float32 [1024], P('fsdp')
- lnp_g: float32 [1024], P('fsdp')
- lnp_b: float32 [1024], P('fsdp')
- ln1_g: float32 [1024], P('fsdp')
- ln1_b: float32 [1024], P('fsdp')
- w_qkv: float32 [1024, 3, 16, 64], P('fsdp')
- b_qkv: float32 [3072], P('fsdp')
- w_out: float32 [1024, 1024], P('fsdp')
- b_out: float32 [1024], P('fsdp')
- ln2_g: float32 [1024], P('fsdp')
- ln2_b: float32 [1024], P('fsdp')
- w_fc: float32 [1024, 4096], P('fsdp')
- b_fc: float32 [4096], P('fsdp')
- w_proj: float32 [4096, 1024], P('fsdp')
- b_proj: float32 [1024], P('fsdp')
- grad_h1: bfloat16 [1024, 50, 1024], P('fsdp')
Outputs:
- output 1: bfloat16 [1024, 50, 1024], P('fsdp')
- output 2: float32 [768, 1024], P(None, 'fsdp')
- output 3: float32 [1024], P('fsdp')
- output 4: float32 [197, 1024], P(None, 'fsdp')
- output 5: float32 [1024], P('fsdp')
- output 6: float32 [1024], P('fsdp')
- output 7: float32 [1024], P('fsdp')
- output 8: float32 [1024], P('fsdp')
- output 9: float32 [1024], P('fsdp')
- output 10: float32 [1024, 3, 16, 64], P('fsdp')
- output 11: float32 [3072], P('fsdp')
- output 12: float32 [1024, 1024], P('fsdp')
- output 13: float32 [1024], P('fsdp')
- output 14: float32 [1024], P('fsdp')
- output 15: float32 [1024], P('fsdp')
- output 16: float32 [1024, 4096], P('fsdp')
- output 17: float32 [4096], P('fsdp')
- output 18: float32 [4096, 1024], P('fsdp')
- output 19: float32 [1024], P('fsdp')
All inputs are finite; a program needn't handle non-finite values.
Results may differ from a plain program's by a relative error of at most 0.02.
Values are sent between devices in bfloat16 or wider.
A program may use at most 1 GiB of HBM per device.

v0:
```python
import functools

import jax
import jax.numpy as jnp
from jax import lax
from jax.experimental import pallas as pl
from jax.experimental.pallas import tpu as pltpu
from jax.sharding import PartitionSpec as P


F32, BF16, I32 = jnp.float32, jnp.bfloat16, jnp.int32
LN_EPS = 1e-5
INV_SQRT2 = 0.7071067811865476
INV_SQRT_2PI = 0.3989422804014327
LOG2E = 1.4426950408889634
MASKED = -1e30
SUBLANES, LANES, HEAD = 8, 128, 64
TOK, FEW, MANY = 50, 4, 8
ROWS, GROWS = FEW * TOK, MANY * TOK
WIN = 112
STARTS = (0, ROWS - WIN)
EDGE = 96
PACK, VEC_ROW = 1024, 976
VEC_AT = VEC_ROW % LANES
N_VEC, VEC_ROWS = 10, 32
B_PATCH, CLS, LNP_G, LNP_B, LN1_G, LN1_B, B_OUT, LN2_G, LN2_B, B_PROJ = range(N_VEC)
STEP = 512
ALL_VMEM = 67043328
ANY = pl.BlockSpec(memory_space=pl.ANY)


def product(dims, left, right):
    return lax.dot_general(left, right, ((dims[:1], dims[1:]), ((), ())), preferred_element_type=F32)


dot = functools.partial(product, (1, 0))
dot_nt = functools.partial(product, (1, 1))
dot_tn = functools.partial(product, (0, 0))


def col_sum(x):
    return jnp.sum(x, axis=0, keepdims=True)


def col_max(x):
    return jnp.max(x, axis=0, keepdims=True)


def row_mean(x):
    return jnp.mean(x, axis=1, keepdims=True)


def row(ref, at):
    return ref[at:at + 1, :]


def iota(shape, axis):
    return lax.broadcasted_iota(I32, shape, axis)


def one_hot(test):
    return test.astype(F32).astype(BF16)


def origin(shape, *_):
    return (0,) * len(shape)


def held(shape):
    return pl.BlockSpec(shape, functools.partial(origin, shape), pipeline_mode=pl.Buffered(1))


def held_cols(n_rows, n_cols, at):
    return pl.BlockSpec((n_rows, n_cols), lambda *_: (0, at // n_cols), pipeline_mode=pl.Buffered(1))


def whole_out(shape):
    return pl.BlockSpec(shape, functools.partial(origin, shape))


def rows_spec(n_rows, width):
    return pl.BlockSpec((n_rows, width), lambda i, *_: (i, 0))


def this_block(n_rows, width, n):
    return pl.BlockSpec((n_rows, width), lambda i: (jnp.minimum(i, n - 1), 0))


def last_block(n_rows, width):
    return pl.BlockSpec((n_rows, width), lambda i: (jnp.maximum(i - 1, 0), 0))


def shaped(shape, dtype=F32):
    return jax.ShapeDtypeStruct(shape, dtype)


def call(kernel, after, args, *, prefetch=(), grid=(1,), in_specs, out_specs, out_shape, scratch_shapes=(), flops, n_bytes=0, partners=None, aliases=()):
    n_in, n_after = len(prefetch) + len(args), len(after)

    def body(*refs):
        return kernel(*refs[:n_in], *refs[n_in + n_after:])

    return pl.pallas_call(
        body,
        grid_spec=pltpu.PrefetchScalarGridSpec(
            num_scalar_prefetch=len(prefetch), grid=grid, in_specs=list(in_specs) + [ANY] * n_after,
            out_specs=out_specs, scratch_shapes=list(scratch_shapes)),
        out_shape=out_shape, input_output_aliases=dict(aliases),
        compiler_params=pltpu.CompilerParams(
            dimension_semantics=(pltpu.ARBITRARY,) * len(grid), vmem_limit_bytes=ALL_VMEM,
            collective_id=partners, has_side_effects=partners is not None),
        cost_estimate=pl.CostEstimate(flops=int(flops), bytes_accessed=int(n_bytes), transcendentals=0),
    )(*prefetch, *args, *after)


MESH_AXIS = 'fsdp'
CHIPS = 8


def device(at):
    return dict(device_id=(at,), device_id_type=pl.DeviceIdType.MESH)


def place():
    me = lax.axis_index(MESH_AXIS)
    core, chip = lax.rem(me, 2), lax.div(me, 2)
    return me, chip, core, me + 1 - 2 * core, [lax.rem(chip + k, CHIPS) for k in range(1, CHIPS)]


def meet(partners):
    barrier = pltpu.get_barrier_semaphore()
    for partner in partners:
        pl.semaphore_signal(barrier, **device(partner))
    pl.semaphore_wait(barrier, len(partners))


def first_step():
    return pl.when(pl.program_id(0) == 0)


def final_step():
    return pl.when(pl.program_id(0) == pl.num_programs(0) - 1)


def staggered(body, refs):
    step, last = pl.program_id(0), pl.num_programs(0) - 1
    pl.when(step == 0)(lambda: body(False, True, *refs))
    pl.when((step > 0) & (step < last))(lambda: body(True, True, *refs))
    pl.when(step == last)(lambda: body(True, False, *refs))


def gather_sems():
    dma = pltpu.SemaphoreType.DMA
    return [dma(()), dma((2 * CHIPS - 1,)), dma((2 * CHIPS - 1,))]


def hosted_gather(own_ref, all_ref, own_sem, send_sem, got_sem):
    me, chip, core, partner, others = place()
    sources = [lax.rem(chip + CHIPS - k, CHIPS) for k in range(1, CHIPS)]

    def rows(owner):
        return all_ref.at[pl.ds(pl.multiple_of(owner * HEAD, HEAD), HEAD)]

    def send(source, owner, to, at):
        return pltpu.make_async_remote_copy(source, rows(owner), send_sem.at[at], got_sem.at[at], **device(to))

    local = pltpu.make_async_copy(own_ref, rows(me), own_sem)
    sent = [send(own_ref, me, partner, 0)] + [send(own_ref, me, 2 * other + core, k + 1) for k, other in enumerate(others)]
    passed = [send(rows(2 * source + core), 2 * source + core, partner, CHIPS + k) for k, source in enumerate(sources)]

    @first_step()
    def _():
        meet([partner] + [2 * other + core for other in others])
        local.start()
        for copy in sent:
            copy.start()

    def finish():
        @final_step()
        def _():
            for arrived, copy in zip(sent[1:], passed):
                arrived.wait_recv()
                copy.start()
            local.wait()
            sent[0].wait_recv()
            for copy in passed:
                copy.wait_recv()
            for copy in sent + passed:
                copy.wait_send()

    return finish


def clear(*refs):
    for ref in refs:
        ref[:] = jnp.zeros_like(ref)


def normalize(x):
    centered = x - row_mean(x)
    inv = lax.rsqrt(row_mean(centered * centered) + LN_EPS)
    return centered * inv, inv


def norm_grad(d_out, x_hat, inv, gain):
    d_hat = d_out * gain
    return inv * (d_hat - row_mean(d_hat) - x_hat * row_mean(d_hat * x_hat))


def image_of(at, n_img=FEW):
    return sum((at >= j * TOK).astype(I32) for j in range(1, n_img))


def is_class(n_rows):
    at = iota((n_rows, 1), 0)
    return at == TOK * image_of(at, n_rows // TOK)


def pack_kernel(wt_ref, pt_ref, *refs):
    *vec_refs, out_ref, rows_ref, pos_ref = refs
    n_pix, n_pos = wt_ref.shape[1], pt_ref.shape[1]
    out_ref[:, :n_pix] = wt_ref[:].astype(BF16)
    out_ref[:, n_pix:n_pix + LANES] = pt_ref[:, :LANES].astype(BF16)
    clear(rows_ref, pos_ref)
    pos_ref[:, :n_pos - LANES] = pt_ref[:, LANES:]
    at = VEC_AT
    for ref in vec_refs:
        for lo in range(0, ref.shape[1], HEAD):
            rows_ref[at:at + 1, :HEAD] = ref[:, lo:lo + HEAD]
            at += 1
    out_ref[:, n_pix + LANES:] = (pos_ref[:] + rows_ref[:].T[:HEAD]).astype(BF16)


def pack_small(wt, pt, vecs):
    args = [wt, pt] + vecs
    shape = (HEAD, PACK)
    return call(pack_kernel, (), args, in_specs=[held(x.shape) for x in args], out_specs=whole_out(shape), out_shape=shaped(shape, BF16),
                scratch_shapes=[pltpu.VMEM((LANES, LANES), F32), pltpu.VMEM((HEAD, LANES), F32)], flops=PACK)


def pick_kernel(keep_ref, patches_ref, g_ref, small_ref, zo_ref, gi_ref, all_ref, pad_ref, move_ref, *sems):
    finish = hosted_gather(small_ref, all_ref, *sems)

    @first_step()
    def _():
        to, source = iota((GROWS, GROWS), 0), iota((GROWS, GROWS), 1)
        move_ref[:] = one_hot(to == lax.rem(source, MANY) * TOK + lax.div(source, MANY))

    n_patch, _, n_pix = patches_ref.shape
    clear(pad_ref)
    pad_ref[:, :TOK - 1] = keep_ref[:].astype(F32)
    image, lane = iota(pad_ref.shape, 0), iota(pad_ref.shape, 1)
    spread = pad_ref[:]
    for b in range(MANY):
        spread = jnp.where(image == b, pltpu.roll(pad_ref[:], TOK * b + 1, 1), spread)
    own = (lane > TOK * image) & (lane < TOK * image + TOK)
    token = col_sum(jnp.where(own, spread + 1.0, 0.0))
    source = col_sum(jnp.where(own, spread * MANY + image.astype(F32), 0.0))
    source = jnp.where(token > 0.0, source, -1.0)
    cols = jnp.where(image == 0, source, token).T[:GROWS].astype(I32)
    source, token = cols[:, :1], cols[:, 1:2]
    pick = one_hot(iota((GROWS, MANY * n_patch), 1) == source)
    zo_ref[:, :n_pix] = dot(pick, patches_ref[:].reshape(MANY * n_patch, n_pix)).astype(BF16)
    zo_ref[:, n_pix:] = one_hot(iota((GROWS, PACK - n_pix), 1) == token)
    gi_ref[:] = dot(move_ref[:], g_ref[:].reshape(GROWS, g_ref.shape[2])).astype(BF16)

    finish()


def pick_rows(keep, patches_t, g_t, small):
    _, n_img, _ = patches_t.shape
    d = g_t.shape[2]
    n_tok = n_img * TOK
    by_image = lambda x: pl.BlockSpec((x.shape[0], MANY, x.shape[2]), lambda i: (0, i, 0))
    return call(pick_kernel, (), (keep, patches_t, g_t, small), grid=(n_img // MANY,),
                in_specs=[rows_spec(MANY, TOK - 1), by_image(patches_t), by_image(g_t), ANY],
                out_specs=[rows_spec(GROWS, PACK), rows_spec(GROWS, d), ANY],
                out_shape=[shaped((n_tok, PACK), BF16), shaped((n_tok, d), BF16), shaped((2 * CHIPS * HEAD, PACK), BF16)],
                scratch_shapes=[pltpu.VMEM((MANY, STEP), F32), pltpu.VMEM((GROWS, GROWS), BF16)] + gather_sems(),
                flops=STEP * patches_t.size, partners=0)


def embed_kernel(zo_ref, wt_ref, hat_ref, a_ref, stat_ref, vec_ref, bq_ref, bf_ref, next_ref, now_ref):
    @first_step()
    def _():
        base = VEC_ROW - VEC_AT
        vec_ref[:] = wt_ref[:, base:base + LANES].astype(F32).T[VEC_AT:VEC_AT + VEC_ROWS]
        at = N_VEC
        for ref in (bq_ref, bf_ref):
            n = ref.shape[1] // vec_ref.shape[1]
            chunk = lambda q: row(vec_ref, at + q % n)[:, q // n * HEAD:(q // n + 1) * HEAD]
            for lo in range(0, ref.shape[1], LANES):
                ref[:, lo:lo + LANES] = jnp.concatenate([chunk(lo // HEAD), chunk(lo // HEAD + 1)], axis=1)
            at += n

    now_ref[:] = next_ref[:]
    next_ref[:] = dot_nt(zo_ref[:], wt_ref[:]) + jnp.where(is_class(GROWS), row(vec_ref, CLS), row(vec_ref, B_PATCH))
    hat, inv = normalize(now_ref[:])
    hat_ref[:] = hat
    h0 = hat * row(vec_ref, LNP_G) + row(vec_ref, LNP_B)
    mean1 = row_mean(h0)
    centered = h0 - mean1
    inv1 = lax.rsqrt(row_mean(centered * centered) + LN_EPS)
    a_ref[:] = (centered * inv1 * row(vec_ref, LN1_G) + row(vec_ref, LN1_B)).astype(BF16)
    lane = iota(stat_ref.shape, 1)
    stat_ref[:] = jnp.where(lane == 0, inv, jnp.where(lane == 1, inv1, mean1))


def embed(zo, small, d_qkv, d_mlp):
    n_tok = zo.shape[0]
    d = small.shape[0]
    n = n_tok // GROWS
    outs = ((VEC_ROWS, d), (1, d_qkv), (1, d_mlp))
    return call(embed_kernel, (), (zo, small), grid=(n + 1,),
                in_specs=[this_block(GROWS, PACK, n), held(small.shape)],
                out_specs=[last_block(GROWS, d), last_block(GROWS, d), last_block(GROWS, LANES)] + [whole_out(s) for s in outs],
                out_shape=[shaped((n_tok, d)), shaped((n_tok, d), BF16), shaped((n_tok, LANES))] + [shaped(s) for s in outs],
                scratch_shapes=[pltpu.VMEM((GROWS, d), F32)] * 2, flops=2 * zo.size * d)


def window_mask(start):
    key, query = (iota((WIN, 2 * WIN), axis) for axis in (0, 1))
    return jnp.where(image_of(key + start) == image_of(lax.rem(query, WIN) + start), 0.0, MASKED)


def set_masks(mask_ref):
    for i, start in enumerate(STARTS):
        mask_ref[i] = window_mask(start)


def split_heads(x):
    first = iota(x.shape, 1) < HEAD
    zero = jnp.zeros_like(x)
    return jnp.concatenate([jnp.where(first, x, zero), jnp.where(first, zero, x)], axis=0)


def join_heads(x):
    return jnp.where(iota((WIN, LANES), 1) < HEAD, x[:WIN], x[WIN:])


def join_windows(lo, hi):
    at = EDGE + SUBLANES
    shift = STARTS[1]
    edge = jnp.where(iota((SUBLANES, LANES), 0) < 2 * TOK - EDGE, lo[EDGE:at], hi[EDGE - shift:at - shift])
    return jnp.concatenate([lo[:EDGE], edge, hi[at - shift:]], axis=0)


def weights_t(logits, mask, scale):
    masked = logits + mask
    e = jnp.exp2((masked - col_max(masked)) * (scale * LOG2E))
    return e * (1.0 / col_sum(e))


def lane_tile(at):
    return slice(at * LANES, (at + 1) * LANES)


def reader(ref):
    return lambda at, i: ref[STARTS[i]:STARTS[i] + WIN, lane_tile(at)]


def every_unit(n_tiles):
    return [(pair, i) for pair in range(n_tiles) for i in range(len(STARTS))]


def window_scratch():
    return pltpu.VMEM((len(STARTS), WIN, 2 * WIN), F32)


def attend_kernel(scale, a_ref, w_ref, b_ref, qkv_ref, o_ref, mask_ref):
    @first_step()
    def _():
        set_masks(mask_ref)

    n_tiles = o_ref.shape[1] // LANES
    a = a_ref[:]
    for lo in range(0, b_ref.shape[1], STEP):
        cols = slice(lo, lo + STEP)
        qkv_ref[:, cols] = (dot(a, w_ref[:, cols]) + b_ref[:, cols]).astype(BF16)
    read, units = reader(qkv_ref), every_unit(n_tiles)
    logits = [dot_nt(read(n_tiles + pair, i), split_heads(read(pair, i))) for pair, i in units]
    probs = [weights_t(x, mask_ref[i], scale).astype(BF16) for x, (_, i) in zip(logits, units)]
    outs = [join_heads(dot_tn(p, read(2 * n_tiles + pair, i))) for p, (pair, i) in zip(probs, units)]
    for lo, hi, (pair, _) in zip(outs[::2], outs[1::2], units[::2]):
        o_ref[:, lane_tile(pair)] = join_windows(lo, hi).astype(BF16)


def attend(a, first, b_qkv, scale):
    n_tok, d = a.shape
    width = b_qkv.shape[1]
    return call(functools.partial(attend_kernel, scale), (), (a, first, b_qkv), grid=(n_tok // ROWS,),
                in_specs=[rows_spec(ROWS, d), held_cols(d, width, 0), held(b_qkv.shape)],
                out_specs=[rows_spec(ROWS, width), rows_spec(ROWS, d)],
                out_shape=[shaped((n_tok, width), BF16), shaped((n_tok, d), BF16)],
                scratch_shapes=[window_scratch()], flops=4 * a.size * width)


def attend_grad_kernel(scale, qkv_ref, dctx_ref, dqkv_ref, bsum_ref, mask_ref):
    @first_step()
    def _():
        set_masks(mask_ref)
        clear(bsum_ref)

    n_tiles = dctx_ref.shape[1] // LANES
    read, read_grad, units = reader(qkv_ref), reader(dctx_ref), every_unit(n_tiles)
    q2 = [split_heads(read(pair, i)) for pair, i in units]
    do2 = [split_heads(read_grad(pair, i)) for pair, i in units]
    logits = [dot_nt(read(n_tiles + pair, i), q) for q, (pair, i) in zip(q2, units)]
    dp = [dot_nt(read(2 * n_tiles + pair, i), do) for do, (pair, i) in zip(do2, units)]
    logits = [x * scale + mask_ref[i] for x, (_, i) in zip(logits, units)]
    e = [jnp.exp2((x - col_max(x)) * LOG2E) for x in logits]
    p = [x * (1.0 / col_sum(x)) for x in e]
    dv = [dot(x.astype(BF16), do) for x, do in zip(p, do2)]
    ds = [(x * (y - col_sum(x * y)) * scale).astype(BF16) for x, y in zip(p, dp)]
    dk = [dot(x, q) for x, q in zip(ds, q2)]
    dq = [join_heads(dot_tn(x, read(n_tiles + pair, i))) for x, (pair, i) in zip(ds, units)]
    for at, (pair, _) in enumerate(units[::2]):
        for part, grads in enumerate((dq, dk, dv)):
            both = join_windows(grads[2 * at], grads[2 * at + 1])
            cols = lane_tile(part * n_tiles + pair)
            dqkv_ref[:, cols] = both.astype(BF16)
            bsum_ref[:, cols] += col_sum(both)


def attend_grad(qkv, d_ctx, scale, after):
    n_tok, width = qkv.shape
    return call(functools.partial(attend_grad_kernel, scale), after, (qkv, d_ctx), grid=(n_tok // ROWS,),
                in_specs=[rows_spec(ROWS, width), rows_spec(ROWS, d_ctx.shape[1])], out_specs=[rows_spec(ROWS, width), whole_out((1, width))],
                out_shape=[shaped((n_tok, width), BF16), shaped((1, width))],
                scratch_shapes=[window_scratch()], flops=3 * d_ctx.size * width)


def erf_cdf(u):
    return 0.5 + 0.5 * lax.erf(u * INV_SQRT2)


def mlp_up_kernel(*refs):
    staggered(mlp_up_step, refs)


def mlp_up_step(with_now, with_next, o_ref, hat_ref, wo_ref, wf_ref, vec_ref, bf_ref, m_ref, c_ref, act_ref, pre_ref, next_ref, now_ref):
    if with_now:
        now_ref[:] = next_ref[:]
        c = now_ref[:]
    if with_next:
        m = hat_ref[:] * row(vec_ref, LNP_G) + row(vec_ref, LNP_B) + dot(o_ref[:], wo_ref[:]) + row(vec_ref, B_OUT)
        m_ref[:] = m
        hat2, _ = normalize(m)
        next_c = (hat2 * row(vec_ref, LN2_G) + row(vec_ref, LN2_B)).astype(BF16)
        c_ref[:] = next_c
    if with_now:
        for lo in range(0, wf_ref.shape[1], STEP):
            cols = slice(lo, lo + STEP)
            u = dot(c, wf_ref[:, cols]) + bf_ref[:, cols]
            pre_ref[:, cols] = u
            act_ref[:, cols] = (u * erf_cdf(u)).astype(BF16)
    if with_next:
        next_ref[:] = next_c


def mlp_up(o, hat, w_fo, vecs, b_fc):
    n_tok, d = o.shape
    f = b_fc.shape[1]
    n = n_tok // GROWS
    return call(mlp_up_kernel, (), (o, hat, w_fo, w_fo, vecs, b_fc), grid=(n + 1,),
                in_specs=[this_block(GROWS, d, n), this_block(GROWS, d, n), held_cols(d, d, f), held_cols(d, f, 0), held(vecs.shape), held(b_fc.shape)],
                out_specs=[this_block(GROWS, d, n), this_block(GROWS, d, n), last_block(GROWS, f), last_block(GROWS, f)],
                out_shape=[shaped((n_tok, d)), shaped((n_tok, d), BF16), shaped((n_tok, f), BF16), shaped((n_tok, f))],
                scratch_shapes=[pltpu.VMEM((GROWS, d), BF16)] * 2, flops=3 * o.size * f)


def mlp_down_kernel(act_ref, m_ref, w_ref, vec_ref, own_ref, h1_ref, all_ref, send_sem, got_sem):
    _, chip, core, _, others = place()
    copies = [pltpu.make_async_remote_copy(own_ref.at[other], all_ref.at[chip], send_sem.at[k], got_sem.at[k], **device(2 * other + core))
              for k, other in enumerate(others)]

    @first_step()
    def _():
        meet([2 * other + core for other in others])
        for copy in copies:
            copy.start()

    h1_ref[:] = (m_ref[:] + dot(act_ref[:], w_ref[:]) + row(vec_ref, B_PROJ)).astype(BF16)

    @final_step()
    def _():
        for copy in copies:
            copy.wait()


def mlp_down(act, m, w_proj, vecs, own, number):
    n_tok, f = act.shape
    d = m.shape[1]
    dma = pltpu.SemaphoreType.DMA((CHIPS - 1,))
    return call(mlp_down_kernel, (), (act, m, w_proj, vecs, own), grid=(n_tok // GROWS,),
                in_specs=[rows_spec(GROWS, f), rows_spec(GROWS, d), held(w_proj.shape), held(vecs.shape), ANY],
                out_specs=[rows_spec(GROWS, d), ANY], out_shape=[shaped((n_tok, d), BF16), shaped(own.shape)], scratch_shapes=[dma, dma],
                flops=2 * m.size * f, partners=number)


def mlp_grad_kernel(g_ref, pre_ref, m_ref, wp_ref, wf_ref, wo_ref, vec_ref, dpre_ref, dmid_ref, dmidb_ref, dctx_ref, vsum_ref, bfc_ref):
    @first_step()
    def _():
        clear(vsum_ref, bfc_ref)

    g = g_ref[:]
    step = 2 * STEP
    d_c = jnp.zeros(m_ref.shape, F32)
    cuts = [slice(lo, lo + step) for lo in range(0, wp_ref.shape[0], step)]
    acts, pres = dict(), dict()
    n = len(cuts)
    for tick in range(n + 2):
        if tick < n:
            acts[tick] = dot_nt(g, wp_ref[cuts[tick], :])
        if 0 <= tick - 1 < n:
            cols = cuts[tick - 1]
            u = pre_ref[:, cols]
            w = u * INV_SQRT2
            d_pre = acts.pop(tick - 1) * (0.5 + 0.5 * lax.erf(w) + u * (jnp.exp2((w * w) * (-LOG2E)) * INV_SQRT_2PI))
            bfc_ref[:, cols] += col_sum(d_pre)
            pres[tick - 1] = d_pre.astype(BF16)
            dpre_ref[:, cols] = pres[tick - 1]
        if tick >= 2:
            d_c = d_c + dot_nt(pres.pop(tick - 2), wf_ref[:, cuts[tick - 2]])
    hat2, inv2 = normalize(m_ref[:])
    g_f = g.astype(F32)
    d_mid = norm_grad(d_c, hat2, inv2, row(vec_ref, LN2_G)) + g_f
    dmid_ref[:] = d_mid
    d_mid_b = d_mid.astype(BF16)
    dmidb_ref[:] = d_mid_b
    dctx_ref[:] = dot_nt(d_mid_b, wo_ref[:]).astype(BF16)
    for at, part in enumerate((d_mid, d_c * hat2, d_c, g_f)):
        vsum_ref[at:at + 1, :] += col_sum(part)


def mlp_grad(g, pre, m, w_proj, w_fo, vecs, after):
    n_tok, d = g.shape
    f = pre.shape[1]
    wide, narrow = rows_spec(GROWS, f), rows_spec(GROWS, d)
    return call(mlp_grad_kernel, after, (g, pre, m, w_proj, w_fo, w_fo, vecs), grid=(n_tok // GROWS,),
                in_specs=[narrow, wide, narrow, held(w_proj.shape), held_cols(d, f, 0), held_cols(d, d, f), held(vecs.shape)],
                out_specs=[wide, narrow, narrow, narrow, whole_out((SUBLANES, d)), whole_out((1, f))],
                out_shape=[shaped((n_tok, f), BF16), shaped((n_tok, d)), shaped((n_tok, d), BF16), shaped((n_tok, d), BF16),
                           shaped((SUBLANES, d)), shaped((1, f))],
                flops=5 * g.size * f)


CUTS = (0, 104, 208, 304, GROWS)


def embed_grad_kernel(*refs):
    @first_step()
    def _():
        clear(refs[7])

    staggered(embed_grad_step, refs)


def embed_grad_step(with_now, with_next, dqkv_ref, dmid_ref, hat_ref, stat_ref, w_ref, vec_ref, demb_ref, vsum_ref, next_ref, now_ref, dx_ref):
    if with_now:
        now_ref[:] = next_ref[:]
    width = now_ref.shape[1] // (len(CUTS) - 1)
    sums = []
    for j, (lo, hi) in enumerate(zip(CUTS, CUTS[1:])):
        cols, rows = slice(j * width, (j + 1) * width), slice(lo, hi)
        if with_next:
            next_ref[:, cols] = dot_nt(dqkv_ref[:], w_ref[cols, :])
        if not with_now:
            continue
        d_a, hat_p = now_ref[rows, :], hat_ref[rows, :]
        inv_p, inv1, mean1 = (stat_ref[rows, k:k + 1] for k in range(3))
        hat1 = (hat_p * row(vec_ref, LNP_G) + row(vec_ref, LNP_B) - mean1) * inv1
        d_zero = norm_grad(d_a, hat1, inv1, row(vec_ref, LN1_G)) + dmid_ref[rows, :]
        d_x = norm_grad(d_zero, hat_p, inv_p, row(vec_ref, LNP_G))
        demb_ref[rows, :] = d_x.astype(BF16)
        dx_ref[rows, :] = d_x
        sums.append([col_sum(part) for part in (d_x, d_zero * hat_p, d_zero, d_a * hat1, d_a)])
    if with_now:
        d_all, *others = (sum(parts) for parts in zip(*sums))
        d_cls = sum(row(dx_ref, at) for at in range(0, GROWS, TOK))
        for at, part in enumerate([d_all - d_cls, d_cls] + others):
            vsum_ref[at:at + 1, :] += part


def embed_grad(dqkv, d_mid, hat, stats, first, vecs, after):
    n_tok, d = d_mid.shape
    width = dqkv.shape[1]
    n = n_tok // GROWS
    return call(embed_grad_kernel, after, (dqkv, d_mid, hat, stats, first, vecs), grid=(n + 1,),
                in_specs=[this_block(GROWS, width, n), last_block(GROWS, d), last_block(GROWS, d), last_block(GROWS, LANES),
                          held_cols(d, width, 0), held(vecs.shape)],
                out_specs=[last_block(GROWS, d), whole_out((SUBLANES, d))], out_shape=[shaped((n_tok, d), BF16), shaped((SUBLANES, d))],
                scratch_shapes=[pltpu.VMEM((GROWS, d), F32)] * 3, flops=3 * d_mid.size * width)


def tail_kernel(se_ref, sm_ref, sq_ref, sf_ref, out_ref, rows_ref):
    d = se_ref.shape[1]
    clear(rows_ref)
    at, cut = VEC_AT, VEC_AT + B_OUT
    rows_ref[at:cut, :] = se_ref[:B_OUT, :]
    at += N_VEC
    rows_ref[cut:at, :] = sm_ref[:N_VEC - B_OUT, :]
    for ref in (sq_ref, sf_ref):
        n = ref.shape[1] // d
        for r in range(n):
            chunk = lambda q: ref[:, (n * q + r) * HEAD:(n * q + r + 1) * HEAD]
            for j in range(d // LANES):
                rows_ref[at:at + 1, lane_tile(j)] = jnp.concatenate([chunk(2 * j), chunk(2 * j + 1)], axis=1)
            at += 1
    for j in range(d // LANES):
        out_ref[lane_tile(j)] = rows_ref[:, lane_tile(j)].T


def vector_tail(*args):
    d = args[0].shape[1]
    return call(tail_kernel, (), args, in_specs=[held(x.shape) for x in args], out_specs=whole_out((d, LANES)), out_shape=shaped((d, LANES)),
                scratch_shapes=[pltpu.VMEM((LANES, d), F32)], flops=d)


RING = [at ^ (at >> 1) for at in range(CHIPS)]


def ring_chip(at):
    half, quarter = lax.div(at, 2), lax.div(at, 4)
    return 4 * quarter + 2 * lax.rem(half + quarter, 2) + lax.rem(at + half, 2)


def wgrad_kernel(by_rows, first_tile, n_in, a_ref, b_ref, *refs):
    out_ref, made_ref, got_ref, own_ref, send_sem, got_sem, free_sem, out_sem, *at_ref = refs[n_in:]
    step, last = pl.program_id(0), pl.num_programs(0) - 1
    slot = lax.rem(step, 2)
    _, _, mine, partner, _ = place()
    partner = device(partner)

    def part(at, core):
        return made_ref.at[at, core] if by_rows else made_ref.at[at, :, core]

    def exchange(at):
        return pltpu.make_async_remote_copy(part(at, 1 - mine), got_ref.at[at], send_sem.at[at], got_sem.at[at], **partner)

    def store(at, tile):
        width = own_ref.shape[-1]
        out = out_ref.at[tile] if by_rows else out_ref.at[:, :, pl.ds(pl.multiple_of((tile + first_tile) * width, width), width)]
        return pltpu.make_async_copy(own_ref.at[at], out, out_sem.at[at])

    def finish(at, tile):
        exchange(at).wait_recv()

        @pl.when(tile >= 2)
        def _():
            store(at, 0).wait()

        own_ref[at] = part(at, mine)[:] + got_ref[at]

        @pl.when(tile + 2 <= last)
        def _():
            pl.semaphore_signal(free_sem.at[at], **partner)

        store(at, tile).start()

    @first_step()
    def _():
        if not by_rows:
            for j in range(CHIPS):
                at_ref[0][lane_tile(RING.index(j)), :] = a_ref[:, lane_tile(j)].T
        meet([partner['device_id'][0]])

    @pl.when(step >= 2)
    def _():
        exchange(slot).wait_send()

    total = dot_tn(a_ref[:], b_ref[:]) if by_rows else dot(at_ref[0][:], b_ref[:])
    made_ref[slot] = total.reshape(made_ref.shape[1:])

    @pl.when(step >= 2)
    def _():
        pl.semaphore_wait(free_sem.at[slot], 1)

    exchange(slot).start()

    @pl.when(step >= 1)
    def _():
        finish(1 - slot, step - 1)

    @pl.when(step == last)
    def _():
        finish(slot, step)
        for at in range(2):
            exchange(at).wait_send()
            store(at, 0).wait()


def wgrad(a, b, number, after, by_rows=False, into=(), spare=0):
    k, m = a.shape
    n = b.shape[1]
    r = m // (2 * CHIPS)
    width = into[0].shape[-1] if into else n + spare
    if by_rows:
        steps, made, own = CHIPS, (2, r, n), (r, n)
        in_specs, scratch = [pl.BlockSpec((k, 2 * r), lambda j: (0, ring_chip(j))), held(b.shape)], []
    else:
        steps, made, own = n // STEP, (CHIPS, 2, r, STEP), (CHIPS, r, STEP)
        in_specs, scratch = [held(a.shape), pl.BlockSpec((k, STEP), lambda j: (0, j))], [pltpu.VMEM((m, k), BF16)]
    slots = lambda shape: pltpu.VMEM((2,) + shape, F32)
    dma = pltpu.SemaphoreType.DMA((2,))
    return call(functools.partial(wgrad_kernel, by_rows, (width - n - spare) // STEP, len(into)), after, (a, b) + tuple(into), grid=(steps,),
                in_specs=in_specs + [ANY] * len(into), out_specs=ANY, out_shape=shaped((CHIPS, r, width)), aliases=[(2, 0)] * len(into),
                scratch_shapes=[slots(made), slots(own), slots(own), dma, dma, pltpu.SemaphoreType.REGULAR((2,)), dma] + scratch,
                flops=2 * k * m * n, partners=number)


def last_kernel(a_ref, b_ref, tail_ref, out_ref, at_ref, made_ref, got_ref, own_ref, swap_sem, out_sem):
    step, n_steps = pl.program_id(0), made_ref.shape[0]
    _, _, core, partner, _ = place()
    width = made_ref.shape[-1]

    def swap(tile):
        return pltpu.make_async_remote_copy(made_ref.at[tile, :, 1 - core], got_ref.at[tile], swap_sem.at[0, tile], swap_sem.at[1, tile], **device(partner))

    def store(tile):
        return pltpu.make_async_copy(own_ref.at[tile], out_ref.at[:, :, pl.ds(pl.multiple_of(tile * width, width), width)], out_sem.at[tile])

    def finish(tile):
        swap(tile).wait_recv()
        own_ref[tile] = made_ref[tile, :, core] + got_ref[tile]
        store(tile).start()

    @first_step()
    def _():
        for j in range(CHIPS):
            at_ref[lane_tile(j), :] = a_ref[:, lane_tile(j)].T
        meet([partner])

    made_ref[step] = dot(at_ref[:], b_ref[:]).reshape(made_ref.shape[1:])

    @final_step()
    def _():
        made_ref[step, :, :, :, width - LANES:] += tail_ref[:].reshape(made_ref.shape[1:4] + (LANES,))

    swap(step).start()

    @pl.when(step > 0)
    def _():
        finish(step - 1)

    @final_step()
    def _():
        finish(step)
        for tile in range(n_steps):
            swap(tile).wait_send()
            store(tile).wait()


def last_grads(a, b, tail, number):
    k, m = a.shape
    n_steps = PACK // STEP
    slots = lambda *shape: pltpu.VMEM((n_steps, CHIPS) + shape + (HEAD, STEP), F32)
    dma = pltpu.SemaphoreType.DMA
    return call(last_kernel, (), (a, b, tail), grid=(n_steps,),
                in_specs=[held(a.shape), pl.BlockSpec((k, STEP), lambda j: (0, j)), held(tail.shape)],
                out_specs=ANY, out_shape=shaped((CHIPS, HEAD, PACK)),
                scratch_shapes=[pltpu.VMEM((m, k), BF16), slots(2), slots(), slots(), dma((2, n_steps)), dma((n_steps,))],
                flops=2 * k * m * PACK, partners=number)


def end_kernel(h1_ref, own_ref, all_ref, token_ref, wt_ref, pos_ref, *refs):
    *vec_refs, full_ref, move_ref = refs

    @first_step()
    def _():
        to, source = iota((GROWS, GROWS), 0), iota((GROWS, GROWS), 1)
        move_ref[:] = one_hot(source == lax.rem(to, MANY) * TOK + lax.div(to, MANY))
        _, chip, _, _, others = place()
        full_ref[:] = own_ref[chip] + sum(all_ref[other] for other in others)
        n_pix, n_pos = wt_ref.shape[1], pos_ref.shape[1]
        wt_ref[:] = full_ref[:, :n_pix]
        pos_ref[:] = full_ref[:, n_pix:n_pix + n_pos]
        pos_ref[:, :1] = full_ref[:, VEC_ROW + CLS:VEC_ROW + CLS + 1]
        rows = full_ref[:, VEC_ROW - VEC_AT:VEC_ROW - VEC_AT + LANES].T
        at = VEC_AT
        for ref in vec_refs:
            for lo in range(0, ref.shape[1], HEAD):
                ref[:, lo:lo + HEAD] = rows[at:at + 1]
                at += 1

    token_ref[:] = dot(move_ref[:], h1_ref[:]).astype(BF16).reshape(token_ref.shape)


def end_grads(h1, own, received, widths):
    n_tok, d = h1.shape
    shapes = [(HEAD, w) for w in widths[:2]] + [(1, w) for w in widths[2:]]
    return call(end_kernel, (), (h1, own, received), grid=(n_tok // GROWS,),
                in_specs=[rows_spec(GROWS, d), held(own.shape), held(received.shape)],
                out_specs=[pl.BlockSpec((TOK, MANY, d), lambda i: (0, i, 0))] + [whole_out(s) for s in shapes],
                out_shape=[shaped((TOK, n_tok // TOK, d), BF16)] + [shaped(s) for s in shapes],
                scratch_shapes=[pltpu.VMEM((HEAD, PACK), F32), pltpu.VMEM((GROWS, GROWS), BF16)], flops=PACK)


PARAM_NAMES = ('w_patch', 'b_patch', 'pos_table', 'cls_tok', 'lnp_g', 'lnp_b', 'ln1_g', 'ln1_b', 'w_qkv', 'b_qkv', 'w_out', 'b_out', 'ln2_g', 'ln2_b', 'w_fc', 'b_fc', 'w_proj', 'b_proj')
PACKED = tuple(PARAM_NAMES[i] for i in (1, 3, 4, 5, 6, 7, 11, 12, 13, 17, 9, 15))


def solution(mesh):
    def compute(patches, keep, *rest):
        shard = dict(zip(PARAM_NAMES, rest[:-1]))
        d, d_mlp = shard['w_out'].shape[1], shard['w_fc'].shape[1]
        n_pix, n_pos = shard['w_patch'].shape[0], shard['pos_table'].shape[0]
        scale = shard['w_qkv'].shape[-1] ** -0.5
        by_token = lambda x: x.transpose(1, 0, 2)

        def whole(value):
            return lax.all_gather(value, MESH_AXIS, tiled=True)

        w_qkv = whole(shard['w_qkv'].astype(BF16).reshape(HEAD, -1))
        small = pack_small(shard['w_patch'].T, shard['pos_table'].T, [shard[name][None] for name in PACKED])
        w_fo = whole(jnp.concatenate([shard['w_fc'].astype(BF16), shard['w_out'].astype(BF16)], axis=1))
        w_proj = whole(shard['w_proj'].astype(BF16))

        zo, g, small = pick_rows(keep, by_token(patches), by_token(rest[-1]), small)
        hat, a, stats, vecs, b_qkv, b_fc = embed(zo, small, w_qkv.shape[1], d_mlp)
        qkv, ctx = attend(a, w_qkv, b_qkv, scale)
        m, c, act, pre = mlp_up(ctx, hat, w_fo, vecs, b_fc)

        def over_chips(made):
            rings = [[2 * chip + core for chip in RING] for core in range(2)]
            return lax.psum_scatter(made.reshape(-1, made.shape[-1]), MESH_AXIS, axis_index_groups=rings, tiled=True)

        made = wgrad(act, g, 2, (), by_rows=True)
        g_proj = over_chips(made)
        d_pre, d_mid, d_mid_b, d_ctx, sums_m, sum_fc = mlp_grad(g, pre, m, w_proj, w_fo, vecs, (made,))
        made = wgrad(c, d_pre, 1, ())
        g_fc = over_chips(made)
        d_qkv, sum_qkv = attend_grad(qkv, d_ctx, scale, (made,))
        made = wgrad(a, d_qkv, 3, (), spare=d)
        made = wgrad(ctx, d_mid_b, 4, (), into=(made,))
        g_qkv_out = over_chips(made)
        d_emb, sums_e = embed_grad(d_qkv, d_mid, hat, stats, w_qkv, vecs, (made,))
        own = last_grads(d_emb, zo, vector_tail(sums_e, sums_m, sum_qkv, sum_fc), 6)
        h1, received = mlp_down(act, m, w_proj, vecs, own, 7)
        widths = [n_pix, n_pos] + [shard[name].shape[0] for name in PACKED]
        h1, *done = end_grads(h1, own, received, widths)

        grads = dict(w_patch=done[0].T, pos_table=done[1].T, w_qkv=g_qkv_out[:, :-d].reshape(shard['w_qkv'].shape), w_out=g_qkv_out[:, -d:], w_fc=g_fc, w_proj=g_proj)
        grads.update({name: value.reshape(-1) for name, value in zip(PACKED, done[2:])})
        return (by_token(h1),) + tuple(grads[name] for name in PARAM_NAMES)

    batch_spec = P(MESH_AXIS)
    param_specs = tuple(P(None, MESH_AXIS) if name in ('w_patch', 'pos_table') else batch_spec for name in PARAM_NAMES)
    return jax.shard_map(compute, mesh=mesh, in_specs=(batch_spec, batch_spec) + param_specs + (batch_spec,), out_specs=(batch_spec,) + param_specs, check_vma=False)
```

profile of v0, /device:TPU:0, one launch (start us, length us, event | category | flops | bytes accessed | tf_op | source)
XLA Modules:
  0.0 726.0 jit_solution(10437355880231878229)
XLA Ops:
  7.2 0.0 copy-start
  7.2 0.0 all-gather.4.cloned.1.call-start
  7.2 1.6 convert_element_type.12
  8.8 1.3 reshape.89
  10.1 0.0 all-gather.4.cloned.1.call-update
  10.1 0.0 all-gather.6.cloned.1.call-start
  10.2 1.0 convert_element_type.14
  11.2 1.3 convert_element_type.13
  12.5 0.9 pad_maximum_fusion
  13.3 0.0 all-gather.6.cloned.1.call-update
  13.4 0.0 all-gather.8.cloned.1.call-start
  13.4 0.0 copy-done
  13.4 0.9 convert_element_type.15
  14.3 0.0 all-gather.8.cloned.1.call-update
  14.3 0.0 reduce-scatter.4.cloned.1.call-start
  14.4 1.9 shard_map.348.refs_3_
  16.2 1.4 copy.41.refs_0_
  17.7 29.6 %shard_map.349 = (bf16[3200,1024]{1,0:T(8,128)(2,1)}, bf16[3200,1024]{1,0:T(8,128)(2,1)}, bf16[1024,1024]{1,0:T(8,128)(2,1)}) custom-call(s32[64,49]{1,0:T(8,128)} %copy.41.refs_0_, bf16[196,64,768]{2,1,0:T(8,128)(2,1)} %bitcast.37, bf16[50,64,1024]{2,1,0:T(8,128)(2,1)} %bitcast.40, bf16[64,1024]{1,0:T(8,128)(2,1)} %shard_map.348.refs_3_), custom_call_target="tpu_custom_call" | custom-call | flops 4932501504 | tf_op jit(solution)/shard_map/pallas_call | solution.py:103
  47.3 20.5 %shard_map.350 = (f32[3200,1024]{1,0:T(8,128)}, bf16[3200,1024]{1,0:T(8,128)(2,1)}, f32[3200,128]{1,0:T(8,128)}, f32[32,1024]{1,0:T(8,128)}, f32[1,3072]{1,0:T(1,128)}, /*index=5*/f32[1,4096]{1,0:T(1,128)}) custom-call(bf16[3200,1024]{1,0:T(8,128)(2,1)} %get-tuple-element.61.refs_0_.refs_1_, bf16[1024,1024]{1,0:T(8,128)(2,1)} %get-tuple-element.62.refs_1_), custom_call_target="tpu_custom_call" | custom-call | flops 6710886400 | tf_op jit(solution)/shard_map/pallas_call | solution.py:103
  67.8 0.0 all-gather.4.cloned.1.call-done.refs_1_.refs_4_
  67.8 45.9 %shard_map.351 = (bf16[3200,3072]{1,0:T(8,128)(2,1)}, bf16[3200,1024]{1,0:T(8,128)(2,1)}) custom-call(bf16[3200,1024]{1,0:T(8,128)(2,1)} %get-tuple-element.63.refs_0_, bf16[1024,3072]{1,0:T(8,128)(2,1)} %all-gather.4.cloned.1.call-done.refs_1_.refs_4_, f32[1,3072]{1,0:T(1,128)} %get-tuple-element.64.refs_2_), custom_call_target="tpu_custom_call" | custom-call | flops 40265318400 | tf_op jit(solution)/shard_map/pallas_call | solution.py:103
  113.7 8.0 %all-gather.6.cloned.1.call-done.refs_2_.refs_3_.refs_4_.refs_5_ = bf16[1024,5120]{1,0:T(8,128)(2,1)} async-done(((bf16[64,5120]{1,0:T(8,128)(2,1)}), bf16[1024,5120]{1,0:T(8,128)(2,1)}) %all-gather.6.cloned.1.call-update) | async-done | bytes 10485776 | tf_op jit(solution)/shard_map/all_gather | solution.py:812
  121.8 54.5 %shard_map.352 = (f32[3200,1024]{1,0:T(8,128)}, bf16[3200,1024]{1,0:T(8,128)(2,1)}, bf16[3200,4096]{1,0:T(8,128)(2,1)}, f32[3200,4096]{1,0:T(8,128)}) custom-call(bf16[3200,1024]{1,0:T(8,128)(2,1)} %get-tuple-element.65.refs_0_, f32[3200,1024]{1,0:T(8,128)} %get-tuple-element.66.refs_1_.refs_2_, ...), custom_call_target="tpu_custom_call" | custom-call | flops 40265318400 | tf_op jit(solution)/shard_map/pallas_call | solution.py:103
  176.3 38.4 %shard_map.353.refs_7_ = f32[8,256,1024]{2,1,0:T(8,128)} custom-call(bf16[3200,4096]{1,0:T(8,128)(2,1)} %get-tuple-element.69.refs_0_, bf16[3200,1024]{1,0:T(8,128)(2,1)} %get-tuple-element.72.refs_1_.refs_0_), custom_call_target="tpu_custom_call" | custom-call | flops 26843545600 | tf_op jit(solution)/shard_map/pallas_call | solution.py:103
  214.7 0.0 all-gather.8.cloned.1.call-done.refs_3_.refs_2_
  214.7 89.1 %shard_map.354 = (bf16[3200,4096]{1,0:T(8,128)(2,1)}, f32[3200,1024]{1,0:T(8,128)}, bf16[3200,1024]{1,0:T(8,128)(2,1)}, bf16[3200,1024]{1,0:T(8,128)(2,1)}, f32[8,1024]{1,0:T(8,128)}, /*index=5*/f32[1,4096]{1,0:T(1,128)}) custom-call(bf16[3200,1024]{1,0:T(8,128)(2,1)} %get-tuple-element.72.refs_1_.refs_0_, f32[3200,4096]{1,0:T(8,128)} %get-tuple-element.73.refs_1_, ...), custom_call_target="tpu_custom_call" | custom-call | flops 67108864000 | tf_op jit(solution)/shard_map/pallas_call | solution.py:103
  303.8 39.9 %shard_map.355.refs_2_ = f32[8,64,4096]{2,1,0:T(8,128)} custom-call(bf16[3200,1024]{1,0:T(8,128)(2,1)} %get-tuple-element.75.refs_0_, bf16[3200,4096]{1,0:T(8,128)(2,1)} %get-tuple-element.76.refs_1_), custom_call_target="tpu_custom_call" | custom-call | flops 26843545600 | tf_op jit(solution)/shard_map/pallas_call | solution.py:103
  343.7 40.9 %shard_map.356 = (bf16[3200,3072]{1,0:T(8,128)(2,1)}, f32[1,3072]{1,0:T(1,128)}) custom-call(bf16[3200,3072]{1,0:T(8,128)(2,1)} %get-tuple-element.71.refs_0_, bf16[3200,1024]{1,0:T(8,128)(2,1)} %get-tuple-element.74.refs_1_, f32[8,64,4096]{2,1,0:T(8,128)} %shard_map.355.refs_2_), custom_call_target="tpu_custom_call" | custom-call | flops 30198988800 | tf_op jit(solution)/shard_map/pallas_call | solution.py:103
  384.7 32.3 %shard_map.357.refs_2_ = f32[8,64,4096]{2,1,0:T(8,128)} custom-call(bf16[3200,1024]{1,0:T(8,128)(2,1)} %get-tuple-element.63.refs_0_, bf16[3200,3072]{1,0:T(8,128)(2,1)} %get-tuple-element.77.refs_1_.refs_0_), custom_call_target="tpu_custom_call" | custom-call | flops 20132659200 | tf_op jit(solution)/shard_map/pallas_call | solution.py:103
  416.9 16.8 %shard_map.358.refs_6_ = f32[8,64,4096]{2,1,0:T(8,128)} custom-call(bf16[3200,1024]{1,0:T(8,128)(2,1)} %get-tuple-element.65.refs_0_, bf16[3200,1024]{1,0:T(8,128)(2,1)} %get-tuple-element.80.refs_1_, f32[8,64,4096]{2,1,0:T(8,128)} %shard_map.357.refs_2_), custom_call_target="tpu_custom_call", output_to_operand_aliasing={{}: (2, {})} | custom-call | flops 6710886400 | tf_op jit(solution)/shard_map/pallas_call | solution.py:103
  433.8 0.0 reduce-scatter.4.cloned.1.call-update
  433.8 0.0 reduce-scatter.8.cloned.1.call-start
  433.8 0.5 reduce-scatter.8.cloned.1.call-update
  434.4 0.0 reduce-scatter.6.cloned.1.call-start
  434.4 0.5 reduce-scatter.6.cloned.1.call-update
  435.0 43.2 %shard_map.359 = (bf16[3200,1024]{1,0:T(8,128)(2,1)}, f32[8,1024]{1,0:T(8,128)}) custom-call(bf16[3200,3072]{1,0:T(8,128)(2,1)} %get-tuple-element.77.refs_1_.refs_0_, f32[3200,1024]{1,0:T(8,128)} %get-tuple-element.78.refs_1_, f32[3200,1024]{1,0:T(8,128)} %get-tuple-element.66.refs_1_.refs_2_, f32[3200,128]{1,0:T(8,128)} %get-tuple-element.79.refs_3_, ...), custom_call_target="tpu_custom_call" | custom-call | flops 30198988800 | tf_op jit(solution)/shard_map/pallas_call | solution.py:103
  478.2 1.9 shard_map.360.refs_2_
  480.0 17.0 %shard_map.361.refs_4_.refs_1_ = f32[8,64,1024]{2,1,0:T(8,128)} custom-call(bf16[3200,1024]{1,0:T(8,128)(2,1)} %get-tuple-element.81.refs_0_, bf16[3200,1024]{1,0:T(8,128)(2,1)} %get-tuple-element.61.refs_0_.refs_1_, f32[1024,128]{1,0:T(8,128)} %shard_map.360.refs_2_), custom_call_target="tpu_custom_call" | custom-call | flops 6710886400 | tf_op jit(solution)/shard_map/pallas_call | solution.py:103
  497.1 44.9 %shard_map.362 = (bf16[3200,1024]{1,0:T(8,128)(2,1)}, f32[8,64,1024]{2,1,0:T(8,128)}) custom-call(bf16[3200,4096]{1,0:T(8,128)(2,1)} %get-tuple-element.69.refs_0_, f32[3200,1024]{1,0:T(8,128)} %get-tuple-element.70.refs_2_.refs_1_, bf16[4096,1024]{1,0:T(8,128)(2,1)} %all-gather.8.cloned.1.call-done.refs_3_.refs_2_, ...), custom_call_target="tpu_custom_call" | custom-call | flops 26843545600 | tf_op jit(solution)/shard_map/pallas_call | solution.py:103
  541.9 11.4 %shard_map.363 = (bf16[50,64,1024]{2,1,0:T(8,128)(2,1)}, f32[64,768]{1,0:T(8,128)}, f32[64,197]{1,0:T(8,128)}, f32[1,64]{1,0:T(1,128)}, f32[1,64]{1,0:T(1,128)},...) custom-call(bf16[3200,1024]{1,0:T(8,128)(2,1)} %get-tuple-element.86, ...), custom_call_target="tpu_custom_call" | custom-call | flops 1024 | tf_op jit(solution)/shard_map/pallas_call | solution.py:103
  553.4 0.0 reduce-scatter.4.cloned.1.call-done
  553.4 1.2 slice.8
  554.6 1.6 reshape.97
  556.1 1.7 slice.9
  557.8 72.2 %reduce-scatter.8.cloned.1.call-done = f32[256,1024]{1,0:T(8,128)} async-done(((f32[2048,1024]{1,0:T(8,128)}), f32[256,1024]{1,0:T(8,128)}) %reduce-scatter.8.cloned.1.call-update) | async-done | bytes 1048592 | tf_op jit(solution)/shard_map/reduce_scatter | solution.py:826
  630.0 88.9 %reduce-scatter.6.cloned.1.call-done = f32[64,4096]{1,0:T(8,128)} async-done(((f32[512,4096]{1,0:T(8,128)}), f32[64,4096]{1,0:T(8,128)}) %reduce-scatter.6.cloned.1.call-update) | async-done | bytes 1048592 | tf_op jit(solution)/shard_map/reduce_scatter | solution.py:826
Async XLA Ops:
  7.2 6.2 copy-start
  7.2 60.6 %all-gather.4.cloned.1.call-start = ((), (), s32[]{:S(2)}) async-start(), calls=%async_computation.3 | async-start | bytes 6684672 | tf_op jit(solution)/shard_map/all_gather | solution.py:812
  10.1 111.6 %all-gather.6.cloned.1.call-start = ((), (), s32[]{:S(2)}) async-start(), calls=%async_computation.4 | async-start | bytes 11141120 | tf_op jit(solution)/shard_map/all_gather | solution.py:812
  13.4 201.3 %all-gather.8.cloned.1.call-start = ((), (), s32[]{:S(2)}) async-start(), calls=%async_computation.5 | async-start | bytes 8912896 | tf_op jit(solution)/shard_map/all_gather | solution.py:812
  14.3 539.0 %reduce-scatter.4.cloned.1.call-start = ((), (), s32[]{:S(2)}) async-start(), calls=%async_computation.6 | async-start | bytes 9437184 | tf_op jit(solution)/shard_map/reduce_scatter | solution.py:826
  433.8 196.2 %reduce-scatter.8.cloned.1.call-start = ((), (), s32[]{:S(2)}) async-start(), calls=%async_computation.8 | async-start | bytes 9437184 | tf_op jit(solution)/shard_map/reduce_scatter | solution.py:826
  434.4 284.6 %reduce-scatter.6.cloned.1.call-start = ((), (), s32[]{:S(2)}) async-start(), calls=%async_computation.7 | async-start | bytes 9437184 | tf_op jit(solution)/shard_map/reduce_scatter | solution.py:826
Sparse Core Ops, SparseCore 0:
  10.8 52.1 all-gather.3
  65.8 55.8 all-gather.5
  124.6 48.9 all-gather.7
  433.9 108.1 reduce-scatter.3
  544.8 85.2 reduce-scatter.7
  632.7 86.1 reduce-scatter.5
where the time goes:
time: 732 us; the launch traced here: 726 us
  Pallas kernels  528 us (72%)
  waiting for transfers between devices  170 us (23%)
  between operations  14.5 us (2%)
    pallas_call x16, Pallas kernels, call(): pl.pallas_call(body, grid_spec=pltpu.PrefetchScalarGridSpec(num_scalar_pr...  528 us
    reduce_scatter x3, waiting for transfers between devices, over_chips(): lax.psum_scatter(made.reshape(-1, made.shape[-1]), MESH_AXIS, axis_index_...  161 us
  transfers between devices with their start and end apart: 6, of which 3 were waited for; matrix products, arithmetic and copies ran while one was open for 1% of the time, Pallas kernels for 43%

commit v1 on v0

--- a/solution.py
+++ b/solution.py
@@ -469,7 +469,7 @@
                 scratch_shapes=[pltpu.VMEM((GROWS, d), BF16)] * 2, flops=3 * o.size * f)
 
 
-def mlp_down_kernel(act_ref, m_ref, w_ref, vec_ref, own_ref, h1_ref, all_ref, send_sem, got_sem):
+def mlp_down_kernel(act_ref, m_ref, w_ref, vec_ref, own_ref, h1_ref, all_ref, move_ref, send_sem, got_sem):
     _, chip, core, _, others = place()
     copies = [pltpu.make_async_remote_copy(own_ref.at[other], all_ref.at[chip], send_sem.at[k], got_sem.at[k], **device(2 * other + core))
               for k, other in enumerate(others)]
@@ -479,8 +479,11 @@
         meet([2 * other + core for other in others])
         for copy in copies:
             copy.start()
-
-    h1_ref[:] = (m_ref[:] + dot(act_ref[:], w_ref[:]) + row(vec_ref, B_PROJ)).astype(BF16)
+        to, source = iota((GROWS, GROWS), 0), iota((GROWS, GROWS), 1)
+        move_ref[:] = one_hot(source == lax.rem(to, MANY) * TOK + lax.div(to, MANY))
+
+    h1 = (m_ref[:] + dot(act_ref[:], w_ref[:]) + row(vec_ref, B_PROJ)).astype(BF16)
+    h1_ref[:] = dot(move_ref[:], h1).astype(BF16).reshape(h1_ref.shape)
 
     @final_step()
     def _():
@@ -494,7 +497,9 @@
     dma = pltpu.SemaphoreType.DMA((CHIPS - 1,))
     return call(mlp_down_kernel, (), (act, m, w_proj, vecs, own), grid=(n_tok // GROWS,),
                 in_specs=[rows_spec(GROWS, f), rows_spec(GROWS, d), held(w_proj.shape), held(vecs.shape), ANY],
-                out_specs=[rows_spec(GROWS, d), ANY], out_shape=[shaped((n_tok, d), BF16), shaped(own.shape)], scratch_shapes=[dma, dma],
+                out_specs=[pl.BlockSpec((TOK, MANY, d), lambda i: (0, i, 0)), ANY],
+                out_shape=[shaped((TOK, n_tok // TOK, d), BF16), shaped(own.shape)],
+                scratch_shapes=[pltpu.VMEM((GROWS, GROWS), BF16), dma, dma],
                 flops=2 * m.size * f, partners=number)
 
 
@@ -764,12 +769,11 @@
 
 
 def end_kernel(h1_ref, own_ref, all_ref, token_ref, wt_ref, pos_ref, *refs):
-    *vec_refs, full_ref, move_ref = refs
-
-    @first_step()
-    def _():
-        to, source = iota((GROWS, GROWS), 0), iota((GROWS, GROWS), 1)
-        move_ref[:] = one_hot(source == lax.rem(to, MANY) * TOK + lax.div(to, MANY))
+    *vec_refs, full_ref = refs
+    token_ref[:] = h1_ref[:]
+
+    @first_step()
+    def _():
         _, chip, _, _, others = place()
         full_ref[:] = own_ref[chip] + sum(all_ref[other] for other in others)
         n_pix, n_pos = wt_ref.shape[1], pos_ref.shape[1]
@@ -783,17 +787,15 @@
                 ref[:, lo:lo + HEAD] = rows[at:at + 1]
                 at += 1
 
-    token_ref[:] = dot(move_ref[:], h1_ref[:]).astype(BF16).reshape(token_ref.shape)
-
 
 def end_grads(h1, own, received, widths):
     n_tok, d = h1.shape
     shapes = [(HEAD, w) for w in widths[:2]] + [(1, w) for w in widths[2:]]
     return call(end_kernel, (), (h1, own, received), grid=(n_tok // GROWS,),
                 in_specs=[rows_spec(GROWS, d), held(own.shape), held(received.shape)],
-                out_specs=[pl.BlockSpec((TOK, MANY, d), lambda i: (0, i, 0))] + [whole_out(s) for s in shapes],
-                out_shape=[shaped((TOK, n_tok // TOK, d), BF16)] + [shaped(s) for s in shapes],
-                scratch_shapes=[pltpu.VMEM((HEAD, PACK), F32), pltpu.VMEM((GROWS, GROWS), BF16)], flops=PACK)
+                out_specs=[rows_spec(GROWS, d)] + [whole_out(s) for s in shapes],
+                out_shape=[shaped((n_tok, d), BF16)] + [shaped(s) for s in shapes],
+                scratch_shapes=[pltpu.VMEM((HEAD, PACK), F32)], flops=PACK)
 
 
 PARAM_NAMES = ('w_patch', 'b_patch', 'pos_table', 'cls_tok', 'lnp_g', 'lnp_b', 'ln1_g', 'ln1_b', 'w_qkv', 'b_qkv', 'w_out', 'b_out', 'ln2_g', 'ln2_b', 'w_fc', 'b_fc', 'w_proj', 'b_proj')
@@ -838,11 +840,11 @@
         own = last_grads(d_emb, zo, vector_tail(sums_e, sums_m, sum_qkv, sum_fc), 6)
         h1, received = mlp_down(act, m, w_proj, vecs, own, 7)
         widths = [n_pix, n_pos] + [shard[name].shape[0] for name in PACKED]
-        h1, *done = end_grads(h1, own, received, widths)
+        by_rows, *done = end_grads(h1.reshape(-1, d), own, received, widths)
 
         grads = dict(w_patch=done[0].T, pos_table=done[1].T, w_qkv=g_qkv_out[:, :-d].reshape(shard['w_qkv'].shape), w_out=g_qkv_out[:, -d:], w_fc=g_fc, w_proj=g_proj)
         grads.update({name: value.reshape(-1) for name, value in zip(PACKED, done[2:])})
-        return (by_token(h1),) + tuple(grads[name] for name in PARAM_NAMES)
+        return (by_token(by_rows.reshape(h1.shape)),) + tuple(grads[name] for name in PARAM_NAMES)
 
     batch_spec = P(MESH_AXIS)
     param_specs = tuple(P(None, MESH_AXIS) if name in ('w_patch', 'pos_table') else batch_spec for name in PARAM_NAMES)

time: 732 us -> 732 us (level)
  transfers between devices with their start and end apart: 6 -> 6, of which waited for: 3 -> 3; matrix products, arithmetic and copies ran while one was open for 1% -> 1% of each run, Pallas kernels for 43% -> 42%
where the time goes in v1:
time: 732 us; the launch traced here: 726 us
  Pallas kernels  527 us (72%)
  waiting for transfers between devices  172 us (23%)
  between operations  14.5 us (2%)
    pallas_call x16, Pallas kernels, call(): pl.pallas_call(body, grid_spec=pltpu.PrefetchScalarGridSpec(num_scalar_pr...  527 us
    reduce_scatter x3, waiting for transfers between devices, over_chips(): lax.psum_scatter(made.reshape(-1, made.shape[-1]), MESH_AXIS, axis_index_...  163 us
  transfers between devices with their start and end apart: 6, of which 3 were waited for; matrix products, arithmetic and copies ran while one was open for 1% of the time, Pallas kernels for 42%

profile of v1, /device:TPU:0, one launch (start us, length us, event | category | flops | bytes accessed | tf_op | source)
XLA Modules:
  0.0 726.0 jit_solution(13900679389743036511)
XLA Ops:
  7.2 0.0 copy-start
  7.2 0.0 all-gather.4.cloned.1.call-start
  7.2 1.6 convert_element_type.12
  8.8 1.3 reshape.95
  10.1 0.0 all-gather.4.cloned.1.call-update
  10.1 0.0 all-gather.6.cloned.1.call-start
  10.2 1.0 convert_element_type.14
  11.2 1.3 convert_element_type.13
  12.5 0.9 pad_maximum_fusion
  13.3 0.0 all-gather.6.cloned.1.call-update
  13.4 0.0 all-gather.8.cloned.1.call-start
  13.4 0.0 copy-done
  13.4 0.9 convert_element_type.15
  14.3 0.0 all-gather.8.cloned.1.call-update
  14.3 0.0 reduce-scatter.4.cloned.1.call-start
  14.4 1.9 shard_map.348.refs_3_
  16.2 1.4 copy.41.refs_0_
  17.7 29.6 %shard_map.349 = (bf16[3200,1024]{1,0:T(8,128)(2,1)}, bf16[3200,1024]{1,0:T(8,128)(2,1)}, bf16[1024,1024]{1,0:T(8,128)(2,1)}) custom-call(s32[64,49]{1,0:T(8,128)} %copy.41.refs_0_, bf16[196,64,768]{2,1,0:T(8,128)(2,1)} %bitcast.40, bf16[50,64,1024]{2,1,0:T(8,128)(2,1)} %bitcast.43, bf16[64,1024]{1,0:T(8,128)(2,1)} %shard_map.348.refs_3_), custom_call_target="tpu_custom_call" | custom-call | flops 4932501504 | tf_op jit(solution)/shard_map/pallas_call | solution.py:103
  47.3 20.5 %shard_map.350 = (f32[3200,1024]{1,0:T(8,128)}, bf16[3200,1024]{1,0:T(8,128)(2,1)}, f32[3200,128]{1,0:T(8,128)}, f32[32,1024]{1,0:T(8,128)}, f32[1,3072]{1,0:T(1,128)}, /*index=5*/f32[1,4096]{1,0:T(1,128)}) custom-call(bf16[3200,1024]{1,0:T(8,128)(2,1)} %get-tuple-element.61.refs_0_.refs_1_, bf16[1024,1024]{1,0:T(8,128)(2,1)} %get-tuple-element.62.refs_1_), custom_call_target="tpu_custom_call" | custom-call | flops 6710886400 | tf_op jit(solution)/shard_map/pallas_call | solution.py:103
  67.8 0.0 all-gather.4.cloned.1.call-done.refs_1_.refs_4_
  67.8 45.9 %shard_map.351 = (bf16[3200,3072]{1,0:T(8,128)(2,1)}, bf16[3200,1024]{1,0:T(8,128)(2,1)}) custom-call(bf16[3200,1024]{1,0:T(8,128)(2,1)} %get-tuple-element.63.refs_0_, bf16[1024,3072]{1,0:T(8,128)(2,1)} %all-gather.4.cloned.1.call-done.refs_1_.refs_4_, f32[1,3072]{1,0:T(1,128)} %get-tuple-element.64.refs_2_), custom_call_target="tpu_custom_call" | custom-call | flops 40265318400 | tf_op jit(solution)/shard_map/pallas_call | solution.py:103
  113.7 8.0 %all-gather.6.cloned.1.call-done.refs_2_.refs_3_.refs_4_.refs_5_ = bf16[1024,5120]{1,0:T(8,128)(2,1)} async-done(((bf16[64,5120]{1,0:T(8,128)(2,1)}), bf16[1024,5120]{1,0:T(8,128)(2,1)}) %all-gather.6.cloned.1.call-update) | async-done | bytes 10485776 | tf_op jit(solution)/shard_map/all_gather | solution.py:814
  121.8 54.5 %shard_map.352 = (f32[3200,1024]{1,0:T(8,128)}, bf16[3200,1024]{1,0:T(8,128)(2,1)}, bf16[3200,4096]{1,0:T(8,128)(2,1)}, f32[3200,4096]{1,0:T(8,128)}) custom-call(bf16[3200,1024]{1,0:T(8,128)(2,1)} %get-tuple-element.65.refs_0_, f32[3200,1024]{1,0:T(8,128)} %get-tuple-element.66.refs_1_.refs_2_, ...), custom_call_target="tpu_custom_call" | custom-call | flops 40265318400 | tf_op jit(solution)/shard_map/pallas_call | solution.py:103
  176.3 38.4 %shard_map.353.refs_7_ = f32[8,256,1024]{2,1,0:T(8,128)} custom-call(bf16[3200,4096]{1,0:T(8,128)(2,1)} %get-tuple-element.69.refs_0_, bf16[3200,1024]{1,0:T(8,128)(2,1)} %get-tuple-element.72.refs_1_.refs_0_), custom_call_target="tpu_custom_call" | custom-call | flops 26843545600 | tf_op jit(solution)/shard_map/pallas_call | solution.py:103
  214.7 0.0 all-gather.8.cloned.1.call-done.refs_3_.refs_2_
  214.7 89.1 %shard_map.354 = (bf16[3200,4096]{1,0:T(8,128)(2,1)}, f32[3200,1024]{1,0:T(8,128)}, bf16[3200,1024]{1,0:T(8,128)(2,1)}, bf16[3200,1024]{1,0:T(8,128)(2,1)}, f32[8,1024]{1,0:T(8,128)}, /*index=5*/f32[1,4096]{1,0:T(1,128)}) custom-call(bf16[3200,1024]{1,0:T(8,128)(2,1)} %get-tuple-element.72.refs_1_.refs_0_, f32[3200,4096]{1,0:T(8,128)} %get-tuple-element.73.refs_1_, ...), custom_call_target="tpu_custom_call" | custom-call | flops 67108864000 | tf_op jit(solution)/shard_map/pallas_call | solution.py:103
  303.8 39.9 %shard_map.355.refs_2_ = f32[8,64,4096]{2,1,0:T(8,128)} custom-call(bf16[3200,1024]{1,0:T(8,128)(2,1)} %get-tuple-element.75.refs_0_, bf16[3200,4096]{1,0:T(8,128)(2,1)} %get-tuple-element.76.refs_1_), custom_call_target="tpu_custom_call" | custom-call | flops 26843545600 | tf_op jit(solution)/shard_map/pallas_call | solution.py:103
  343.7 40.9 %shard_map.356 = (bf16[3200,3072]{1,0:T(8,128)(2,1)}, f32[1,3072]{1,0:T(1,128)}) custom-call(bf16[3200,3072]{1,0:T(8,128)(2,1)} %get-tuple-element.71.refs_0_, bf16[3200,1024]{1,0:T(8,128)(2,1)} %get-tuple-element.74.refs_1_, f32[8,64,4096]{2,1,0:T(8,128)} %shard_map.355.refs_2_), custom_call_target="tpu_custom_call" | custom-call | flops 30198988800 | tf_op jit(solution)/shard_map/pallas_call | solution.py:103
  384.7 32.3 %shard_map.357.refs_2_ = f32[8,64,4096]{2,1,0:T(8,128)} custom-call(bf16[3200,1024]{1,0:T(8,128)(2,1)} %get-tuple-element.63.refs_0_, bf16[3200,3072]{1,0:T(8,128)(2,1)} %get-tuple-element.77.refs_1_.refs_0_), custom_call_target="tpu_custom_call" | custom-call | flops 20132659200 | tf_op jit(solution)/shard_map/pallas_call | solution.py:103
  416.9 16.8 %shard_map.358.refs_6_ = f32[8,64,4096]{2,1,0:T(8,128)} custom-call(bf16[3200,1024]{1,0:T(8,128)(2,1)} %get-tuple-element.65.refs_0_, bf16[3200,1024]{1,0:T(8,128)(2,1)} %get-tuple-element.80.refs_1_, f32[8,64,4096]{2,1,0:T(8,128)} %shard_map.357.refs_2_), custom_call_target="tpu_custom_call", output_to_operand_aliasing={{}: (2, {})} | custom-call | flops 6710886400 | tf_op jit(solution)/shard_map/pallas_call | solution.py:103
  433.8 0.0 reduce-scatter.4.cloned.1.call-update
  433.8 0.0 reduce-scatter.8.cloned.1.call-start
  433.8 0.5 reduce-scatter.8.cloned.1.call-update
  434.4 0.0 reduce-scatter.6.cloned.1.call-start
  434.4 0.5 reduce-scatter.6.cloned.1.call-update
  435.0 43.2 %shard_map.359 = (bf16[3200,1024]{1,0:T(8,128)(2,1)}, f32[8,1024]{1,0:T(8,128)}) custom-call(bf16[3200,3072]{1,0:T(8,128)(2,1)} %get-tuple-element.77.refs_1_.refs_0_, f32[3200,1024]{1,0:T(8,128)} %get-tuple-element.78.refs_1_, f32[3200,1024]{1,0:T(8,128)} %get-tuple-element.66.refs_1_.refs_2_, f32[3200,128]{1,0:T(8,128)} %get-tuple-element.79.refs_3_, ...), custom_call_target="tpu_custom_call" | custom-call | flops 30198988800 | tf_op jit(solution)/shard_map/pallas_call | solution.py:103
  478.2 1.9 shard_map.360.refs_2_
  480.0 17.0 %shard_map.361.refs_4_.refs_1_ = f32[8,64,1024]{2,1,0:T(8,128)} custom-call(bf16[3200,1024]{1,0:T(8,128)(2,1)} %get-tuple-element.81.refs_0_, bf16[3200,1024]{1,0:T(8,128)(2,1)} %get-tuple-element.61.refs_0_.refs_1_, f32[1024,128]{1,0:T(8,128)} %shard_map.360.refs_2_), custom_call_target="tpu_custom_call" | custom-call | flops 6710886400 | tf_op jit(solution)/shard_map/pallas_call | solution.py:103
  497.1 44.9 %shard_map.362 = (bf16[50,64,1024]{2,1,0:T(8,128)(2,1)}, f32[8,64,1024]{2,1,0:T(8,128)}) custom-call(bf16[3200,4096]{1,0:T(8,128)(2,1)} %get-tuple-element.69.refs_0_, f32[3200,1024]{1,0:T(8,128)} %get-tuple-element.70.refs_2_.refs_1_, bf16[4096,1024]{1,0:T(8,128)(2,1)} %all-gather.8.cloned.1.call-done.refs_3_.refs_2_, ...), custom_call_target="tpu_custom_call" | custom-call | flops 26843545600 | tf_op jit(solution)/shard_map/pallas_call | solution.py:103
  542.0 9.8 %shard_map.363 = (bf16[3200,1024]{1,0:T(8,128)(2,1)}, f32[64,768]{1,0:T(8,128)}, f32[64,197]{1,0:T(8,128)}, f32[1,64]{1,0:T(1,128)}, f32[1,64]{1,0:T(1,128)}, /*...) custom-call(bf16[3200,1024]{1,0:T(8,128)(2,1)} %bitcast.44, ...), custom_call_target="tpu_custom_call" | custom-call | flops 1024 | tf_op jit(solution)/shard_map/pallas_call | solution.py:103
  551.8 0.0 reduce-scatter.4.cloned.1.call-done
  551.8 1.2 slice.8
  553.0 1.6 reshape.105
  554.5 1.7 slice.9
  556.2 73.8 %reduce-scatter.8.cloned.1.call-done = f32[256,1024]{1,0:T(8,128)} async-done(((f32[2048,1024]{1,0:T(8,128)}), f32[256,1024]{1,0:T(8,128)}) %reduce-scatter.8.cloned.1.call-update) | async-done | bytes 1048592 | tf_op jit(solution)/shard_map/reduce_scatter | solution.py:828
  630.0 88.9 %reduce-scatter.6.cloned.1.call-done = f32[64,4096]{1,0:T(8,128)} async-done(((f32[512,4096]{1,0:T(8,128)}), f32[64,4096]{1,0:T(8,128)}) %reduce-scatter.6.cloned.1.call-update) | async-done | bytes 1048592 | tf_op jit(solution)/shard_map/reduce_scatter | solution.py:828
Async XLA Ops:
  7.2 6.2 copy-start
  7.2 60.6 %all-gather.4.cloned.1.call-start = ((), (), s32[]{:S(2)}) async-start(), calls=%async_computation.3 | async-start | bytes 6684672 | tf_op jit(solution)/shard_map/all_gather | solution.py:814
  10.1 111.6 %all-gather.6.cloned.1.call-start = ((), (), s32[]{:S(2)}) async-start(), calls=%async_computation.4 | async-start | bytes 11141120 | tf_op jit(solution)/shard_map/all_gather | solution.py:814
  13.4 201.3 %all-gather.8.cloned.1.call-start = ((), (), s32[]{:S(2)}) async-start(), calls=%async_computation.5 | async-start | bytes 8912896 | tf_op jit(solution)/shard_map/all_gather | solution.py:814
  14.3 537.5 %reduce-scatter.4.cloned.1.call-start = ((), (), s32[]{:S(2)}) async-start(), calls=%async_computation.6 | async-start | bytes 9437184 | tf_op jit(solution)/shard_map/reduce_scatter | solution.py:828
  433.8 196.2 %reduce-scatter.8.cloned.1.call-start = ((), (), s32[]{:S(2)}) async-start(), calls=%async_computation.8 | async-start | bytes 9437184 | tf_op jit(solution)/shard_map/reduce_scatter | solution.py:828
  434.4 284.6 %reduce-scatter.6.cloned.1.call-start = ((), (), s32[]{:S(2)}) async-start(), calls=%async_computation.7 | async-start | bytes 9437184 | tf_op jit(solution)/shard_map/reduce_scatter | solution.py:828
Sparse Core Ops, SparseCore 0:
  10.8 52.1 all-gather.3
  65.8 55.8 all-gather.5
  124.6 48.9 all-gather.7
  433.9 108.1 reduce-scatter.3
  544.8 85.2 reduce-scatter.7
  632.7 86.1 reduce-scatter.5
